TPU v7x, 512 devices: a whole 4x8x8 slice. The times are simulated.
512 devices in a mesh: frag: 64 (over y, z_hi, core), band: 8 (over x, z_lo).
Axes of the slice: x: 4, y: 8, z: 8 (z_hi: 4, z_lo: 2; z = z_hi * 2 + z_lo), core: 2. Of those that a mesh axis runs over, the one named last changes fastest.
Arguments:
- orbitals: bfloat16 [16384, 32768], P(('frag', 'band')), parts along dimension 0, may hold values from -40 to 40
- potential: float32 [2097152], P('frag'), parts along dimension 0, may hold values from 0.5 to 3
Outputs:
- margin: float32 [16384, 256], P(('frag', 'band')), parts along dimension 0
- projected: float32 [16384, 256], P(('frag', 'band')), parts along dimension 0
- residuals: bfloat16 [16384, 32768], P(('frag', 'band')), parts along dimension 0
There are 64 independent parts, one for each index of `frag`. A program takes and returns all parts, laid end to end along the dimension named above; each array names one. Nothing has to cross between parts.
All inputs are finite; a program needn't handle non-finite values.
Results may differ from a plain program's by a relative error of at most 0.034.
Values may be sent and summed in bfloat16 or wider, within the bound.
A program may use at most 128 MiB of HBM per device.

v0:
```python
import jax
import jax.numpy as jnp
from jax import lax
from jax.sharding import PartitionSpec as P

NSIDE = 32


def from_everyone(shard, axis):
    copies = jnp.broadcast_to(shard, (lax.axis_size(axis), *shard.shape))
    return lax.all_to_all(copies, axis, split_axis=0, concat_axis=0, tiled=True)


def taken_together(shard, axis):
    return from_everyone(shard, axis).astype(jnp.float32).sum(axis=0)


def plane_table(side):
    cells = side * side
    row_index = lax.broadcasted_iota(jnp.int32, (cells, cells), 0)
    col_index = lax.broadcasted_iota(jnp.int32, (cells, cells), 1)
    row_y = row_index // side
    row_z = row_index % side
    col_y = col_index // side
    col_z = col_index % side
    same_y = row_y == col_y
    same_z = row_z == col_z
    near_y = same_z & (((row_y + 1) % side == col_y) | ((col_y + 1) % side == row_y))
    near_z = same_y & (((row_z + 1) % side == col_z) | ((col_z + 1) % side == row_z))
    table = (
        jnp.where(same_y & same_z, 4.0, 0.0)
        - jnp.where(near_y, 1.0, 0.0)
        - jnp.where(near_z, 1.0, 0.0)
    )
    return table.astype(jnp.bfloat16)


def apply_hamiltonian(orbitals, potential):
    count = orbitals.shape[0]
    side = NSIDE
    planes = orbitals.reshape(count * side, side * side)
    plane_part = jnp.dot(planes, plane_table(side), preferred_element_type=jnp.float32)
    plane_part = plane_part.reshape(count, side, side * side)
    stacked = orbitals.reshape(count, side, side * side)
    line_part = (
        2.0 * stacked.astype(jnp.float32)
        - jnp.roll(stacked, 1, 1).astype(jnp.float32)
        - jnp.roll(stacked, -1, 1).astype(jnp.float32)
    )
    pot = potential.reshape(1, side, side * side)
    result = 0.5 * (plane_part + line_part) + pot * stacked.astype(jnp.float32)
    return result.reshape(count, side * side * side).astype(jnp.bfloat16)


def contract_rows(left, right):
    return lax.dot_general(
        left, right, (((1,), (1,)), ((), ())), preferred_element_type=jnp.float32
    )


def shards(orbitals, potential):
    own_count = orbitals.shape[0]
    applied = apply_hamiltonian(orbitals, potential)
    offset = lax.axis_index("band") * own_count
    cell_orbitals, cell_applied = (
        lax.all_to_all(orbitals, "band", split_axis=1, concat_axis=0, tiled=True),
        lax.all_to_all(applied, "band", split_axis=1, concat_axis=0, tiled=True),
    )
    margin_full, projected_full = (
        taken_together(
            contract_rows(cell_orbitals, cell_orbitals).astype(jnp.bfloat16), "band"
        ).astype(jnp.float32),
        taken_together(
            contract_rows(cell_applied, cell_orbitals).astype(jnp.bfloat16), "band"
        ).astype(jnp.float32),
    )
    diagonal = jnp.diagonal(margin_full)
    coefficients = (projected_full / diagonal[:, None]).astype(jnp.bfloat16)
    mixed = jnp.dot(coefficients, cell_orbitals, preferred_element_type=jnp.float32)
    cell_residuals = (cell_applied.astype(jnp.float32) - mixed).astype(jnp.bfloat16)
    residuals = lax.all_to_all(cell_residuals, "band", split_axis=0, concat_axis=1, tiled=True)
    margin = lax.dynamic_slice_in_dim(margin_full, offset, own_count, 0)
    projected = lax.dynamic_slice_in_dim(projected_full, offset, own_count, 0)
    return (margin, projected, residuals)


def solution(mesh):
    return jax.shard_map(
        shards,
        mesh=mesh,
        in_specs=(P(("frag", "band"), None), P("frag")),
        out_specs=(P(("frag", "band"), None), P(("frag", "band"), None), P(("frag", "band"), None)),
        check_vma=False,
    )
```

profile of v0, /device:TPU:168, one launch (start us, length us, event | category | flops | bytes accessed | tf_op | source)
XLA Modules:
  0.0 159.9 jit_solution(7898450948552595136)
XLA Ops:
  0.6 3.3 %copy.35 = bf16[4,8,8,4096]{3,2,0,1:T(8,128)(2,1)} copy(bf16[4,8,8,4096]{3,2,1,0:T(8,128)(2,1)} %bitcast.33) | data formatting | bytes 4194304 | tf_op jit(solution)/shard_map/all_to_all | solution.py:66
  3.9 6.1 %all-to-all-start = ((bf16[32,8,4096]{2,0,1:T(8,128)(2,1)}), bf16[32,8,4096]{2,0,1:T(8,128)(2,1)}, u32[]{:S(2)}, u32[]{:S(2)}) async-start(bf16[32,8,4096]{2,0,1:T(8,128)(2,1)} %bitcast.42), calls=%async_computation | async-start | bytes 4194304 | tf_op jit(solution)/shard_map/all_to_all | solution.py:66
  10.0 1.2 copy.29
  11.2 3.3 %fusion.61 = (bf16[32,31,1024]{2,1,0:T(8,128)(2,1)}, bf16[32,31,1024]{2,1,0:T(8,128)(2,1)}) fusion(bf16[32,32,1024]{2,1,0:T(8,128)(2,1)S(1)} %bitcast.35), kind=kLoop, calls=%fused_computation.101 | loop fusion | bytes 8126464 | tf_op jit(solution)/shard_map/jit(_roll_static)/slice | solution.py:47
  14.5 0.2 fusion.60
  14.7 2.4 %reshape.37 = bf16[1024,1024]{1,0:T(8,128)(2,1)} reshape(bf16[32,32768]{1,0:T(8,128)(2,1)S(1)} %copy-done) | data formatting | bytes 4194304 | tf_op jit(solution)/shard_map/reshape | solution.py:41
  17.1 3.6 %maximum_convert_fusion = (f32[32,32,1024]{2,1,0:T(8,128)S(1)}, f32[32,32,1024]{2,1,0:T(8,128)S(1)}) fusion(bf16[32,31,1024]{2,1,0:T(8,128)(2,1)} %get-tuple-element.5, bf16[32,1,1024]{2,1,0:T(2,128)(2,1)S(1)} %get-tuple-element.3, bf16[32,1,1024]{2,1,0:T(2,128)(2,1)S(1)} %get-tuple-element.4, bf16[32,31,1024]{2,1,0:T(8,128)(2,1)} %get-tuple-element.6), kind=kLoop, calls=%fused_computation.53 | loop fusion | flops 8388608 | bytes 12582912 | tf_op jit(solution)/shard_map/convert_element_type | solution.py:47
  20.8 4.4 %copy.30 = f32[4,8,32,1024]{3,1,2,0:T(8,128)} copy(f32[4,8,32,1024]{3,2,1,0:T(8,128)S(1)} %bitcast.38) | data formatting | bytes 8388608
  25.2 4.4 %copy.31 = f32[4,8,32,1024]{3,1,2,0:T(8,128)} copy(f32[4,8,32,1024]{3,2,1,0:T(8,128)S(1)} %bitcast.37) | data formatting | bytes 8388608
  29.6 7.1 %convolution_bitcast_fusion = f32[1024,1024]{0,1:T(8,128)} fusion(bf16[1024,1024]{1,0:T(8,128)(2,1)S(1)} %copy-done.1, s32[1024]{0:T(1024)S(1)} %get-tuple-element.8, s32[1024]{0:T(1024)S(1)} %get-tuple-element.9, s32[1024]{0:T(1024)S(1)} %get-tuple-element.7, s32[1024]{0:T(1024)S(1)} %get-tuple-element.10, pred[1024]{0:T(1024)(128)(4,1)S(1)} %get-tuple-element.11, ...), kind=kOutput, calls=%fused_computation.50 | convolution fusion | flops 2219835392 | bytes 6309888 | tf_op jit(solution)/shard_map/dot_general | solution.py:42
  36.7 5.3 %copy.23 = f32[1024,1024]{1,0:T(8,128)} copy(f32[1024,1024]{0,1:T(8,128)} %convolution_bitcast_fusion) | data formatting | bytes 8388608 | tf_op jit(solution)/shard_map/dot_general | solution.py:42
  42.0 5.0 %reshape.38 = f32[32,32768]{1,0:T(8,128)} reshape(f32[1024,1024]{1,0:T(8,128)} %copy.23) | data formatting | bytes 8388608 | tf_op jit(solution)/shard_map/reshape | solution.py:43
  47.1 5.8 %fusion.18 = bf16[32,32768]{1,0:T(8,128)(2,1)S(1)} fusion(f32[32,32768]{1,0:T(8,128)} %reshape.38, f32[32,32768]{1,0:T(8,128)} %bitcast.40, f32[32,32768]{1,0:T(8,128)} %bitcast.39, bf16[32,32768]{1,0:T(8,128)(2,1)S(1)} %copy-done, f32[32768]{0:T(1024)S(1)} %copy-done.2), kind=kLoop, calls=%fused_computation.40 | loop fusion | flops 9437184 | bytes 16908288 | tf_op jit(solution)/shard_map/convert_element_type | solution.py:52
  52.9 1.5 copy.34
  54.3 5.7 %all-to-all-start.2 = ((bf16[32,8,4096]{2,0,1:T(8,128)(2,1)}), bf16[32,8,4096]{2,0,1:T(8,128)(2,1)S(1)}, u32[]{:S(2)}, u32[]{:S(2)}) async-start(bf16[32,8,4096]{2,0,1:T(8,128)(2,1)} %bitcast.31), calls=%async_computation.2 | async-start | bytes 4194304 | tf_op jit(solution)/shard_map/all_to_all | solution.py:67
  60.0 3.0 %convolution_convert_fusion.1 = bf16[256,256]{1,0:T(8,128)(2,1)S(1)} fusion(bf16[256,4096]{1,0:T(8,128)(2,1)} %bitcast.1), kind=kOutput, calls=%fused_computation.77 | convolution fusion | flops 536936448 | bytes 2228224 | tf_op jit(solution)/shard_map/dot_general | solution.py:56
  63.0 23.5 %all-to-all-done.2 = bf16[32,8,4096]{2,0,1:T(8,128)(2,1)S(1)} async-done(((bf16[32,8,4096]{2,0,1:T(8,128)(2,1)}), bf16[32,8,4096]{2,0,1:T(8,128)(2,1)S(1)}, u32[]{:S(2)}, u32[]{:S(2)}) %all-to-all-start.2) | async-done | bytes 2097184 | tf_op jit(solution)/shard_map/all_to_all | solution.py:67
  86.4 1.0 broadcast_in_dim.25
  87.5 3.6 %all-to-all-start.1 = ((bf16[8,256,256]{2,1,0:T(8,128)(2,1)}), bf16[8,256,256]{2,1,0:T(8,128)(2,1)S(1)}, u32[]{:S(2)}, u32[]{:S(2)}) async-start(bf16[8,256,256]{2,1,0:T(8,128)(2,1)} %broadcast_in_dim.25), calls=%async_computation.1 | async-start | bytes 2097152 | tf_op jit(solution)/shard_map/all_to_all | solution.py:11
  91.1 2.5 %convolution_convert_fusion = bf16[256,256]{1,0:T(8,128)(2,1)S(1)} fusion(bf16[256,4096]{1,0:T(8,128)(2,1)S(1)} %bitcast.44, bf16[256,4096]{1,0:T(8,128)(2,1)} %bitcast.1), kind=kOutput, calls=%fused_computation.76 | convolution fusion | flops 536936448 | bytes 4325376 | tf_op jit(solution)/shard_map/dot_general | solution.py:56
  93.6 12.5 %all-to-all-done.1 = bf16[8,256,256]{2,1,0:T(8,128)(2,1)S(1)} async-done(((bf16[8,256,256]{2,1,0:T(8,128)(2,1)}), bf16[8,256,256]{2,1,0:T(8,128)(2,1)S(1)}, u32[]{:S(2)}, u32[]{:S(2)}) %all-to-all-start.1) | async-done | bytes 1048608 | tf_op jit(solution)/shard_map/all_to_all | solution.py:11
  106.1 1.0 broadcast_in_dim.29
  107.1 4.2 %all-to-all-start.3 = ((bf16[8,256,256]{2,1,0:T(8,128)(2,1)}), bf16[8,256,256]{2,1,0:T(8,128)(2,1)}, u32[]{:S(2)}, u32[]{:S(2)}) async-start(bf16[8,256,256]{2,1,0:T(8,128)(2,1)} %broadcast_in_dim.29), calls=%async_computation.3 | async-start | bytes 2097152 | tf_op jit(solution)/shard_map/all_to_all | solution.py:11
  111.5 2.3 %gather_fusion = f32[256]{0:T(256)S(1)} fusion(f32[256,256]{1,0:T(8,128)S(1)} %convert_reduce_fusion.1, s32[256]{0:T(256)S(1)} %bitcast.41), kind=kCustom, calls=%fused_computation | custom fusion | bytes 4096 | tf_op jit(solution)/shard_map/jit(diagonal)/cond/branch_0_fun/gather | solution.py:77
  113.9 11.5 %all-to-all-done.3 = bf16[8,256,256]{2,1,0:T(8,128)(2,1)} async-done(((bf16[8,256,256]{2,1,0:T(8,128)(2,1)}), bf16[8,256,256]{2,1,0:T(8,128)(2,1)}, u32[]{:S(2)}, u32[]{:S(2)}) %all-to-all-start.3) | async-done | bytes 1048608 | tf_op jit(solution)/shard_map/all_to_all | solution.py:11
  125.4 1.4 convert_reduce_fusion
  126.8 3.7 %fusion.12 = bf16[256,4096]{1,0:T(8,128)(2,1)} fusion(bf16[256,4096]{1,0:T(8,128)(2,1)} %bitcast.1, bf16[256,4096]{1,0:T(8,128)(2,1)S(1)} %bitcast.45, f32[256,256]{1,0:T(8,128)S(1)} %convert_reduce_fusion, f32[256]{0:T(256)S(1)} %gather_fusion), kind=kOutput, calls=%fused_computation.34 | convolution fusion | flops 540147712 | bytes 6554624 | tf_op jit(solution)/shard_map/dot_general | solution.py:79
  130.5 3.6 %all-to-all-start.4 = ((bf16[8,32,4096]{2,1,0:T(8,128)(2,1)}), bf16[8,32,4096]{2,1,0:T(8,128)(2,1)S(1)}, u32[]{:S(2)}, u32[]{:S(2)}) async-start(bf16[8,32,4096]{2,1,0:T(8,128)(2,1)} %bitcast.46), calls=%async_computation.4 | async-start | bytes 4194304 | tf_op jit(solution)/shard_map/all_to_all | solution.py:81
  134.1 0.6 constant_dynamic-slice_fusion
  134.7 0.6 constant_dynamic-slice_fusion.1
  135.3 23.1 %all-to-all-done.4 = bf16[8,32,4096]{2,1,0:T(8,128)(2,1)S(1)} async-done(((bf16[8,32,4096]{2,1,0:T(8,128)(2,1)}), bf16[8,32,4096]{2,1,0:T(8,128)(2,1)S(1)}, u32[]{:S(2)}, u32[]{:S(2)}) %all-to-all-start.4) | async-done | bytes 2097184 | tf_op jit(solution)/shard_map/all_to_all | solution.py:81
  158.4 1.5 copy.28
  (12 shorter events, 0.2 us)
Async XLA Ops:
  0.6 9.4 %copy-start = (bf16[32,32768]{1,0:T(8,128)(2,1)S(1)}, bf16[32,32768]{1,0:T(8,128)(2,1)}, u32[]{:S(2)}) copy-start(bf16[32,32768]{1,0:T(8,128)(2,1)} %param.2) | copy-start | bytes 6291460
  3.9 50.4 %all-to-all-start = ((bf16[32,8,4096]{2,0,1:T(8,128)(2,1)}), bf16[32,8,4096]{2,0,1:T(8,128)(2,1)}, u32[]{:S(2)}, u32[]{:S(2)}) async-start(bf16[32,8,4096]{2,0,1:T(8,128)(2,1)} %bitcast.42), calls=%async_computation | async-start | bytes 4194304 | tf_op jit(solution)/shard_map/all_to_all | solution.py:66
  25.2 4.4 %copy-start.1 = (bf16[1024,1024]{1,0:T(8,128)(2,1)S(1)}, bf16[1024,1024]{1,0:T(8,128)(2,1)}, u32[]{:S(2)}) copy-start(bf16[1024,1024]{1,0:T(8,128)(2,1)} %reshape.37) | copy-start | bytes 6291460
  42.0 5.0 %copy-start.2 = (f32[32768]{0:T(1024)S(1)}, f32[32768]{0:T(1024)}, u32[]{:S(2)}) copy-start(f32[32768]{0:T(1024)} %param.3) | copy-start | bytes 393220
  54.3 32.1 %all-to-all-start.2 = ((bf16[32,8,4096]{2,0,1:T(8,128)(2,1)}), bf16[32,8,4096]{2,0,1:T(8,128)(2,1)S(1)}, u32[]{:S(2)}, u32[]{:S(2)}) async-start(bf16[32,8,4096]{2,0,1:T(8,128)(2,1)} %bitcast.31), calls=%async_computation.2 | async-start | bytes 4194304 | tf_op jit(solution)/shard_map/all_to_all | solution.py:67
  87.5 18.6 %all-to-all-start.1 = ((bf16[8,256,256]{2,1,0:T(8,128)(2,1)}), bf16[8,256,256]{2,1,0:T(8,128)(2,1)S(1)}, u32[]{:S(2)}, u32[]{:S(2)}) async-start(bf16[8,256,256]{2,1,0:T(8,128)(2,1)} %broadcast_in_dim.25), calls=%async_computation.1 | async-start | bytes 2097152 | tf_op jit(solution)/shard_map/all_to_all | solution.py:11
  107.1 18.3 %all-to-all-start.3 = ((bf16[8,256,256]{2,1,0:T(8,128)(2,1)}), bf16[8,256,256]{2,1,0:T(8,128)(2,1)}, u32[]{:S(2)}, u32[]{:S(2)}) async-start(bf16[8,256,256]{2,1,0:T(8,128)(2,1)} %broadcast_in_dim.29), calls=%async_computation.3 | async-start | bytes 2097152 | tf_op jit(solution)/shard_map/all_to_all | solution.py:11
  130.5 27.9 %all-to-all-start.4 = ((bf16[8,32,4096]{2,1,0:T(8,128)(2,1)}), bf16[8,32,4096]{2,1,0:T(8,128)(2,1)S(1)}, u32[]{:S(2)}, u32[]{:S(2)}) async-start(bf16[8,32,4096]{2,1,0:T(8,128)(2,1)} %bitcast.46), calls=%async_computation.4 | async-start | bytes 4194304 | tf_op jit(solution)/shard_map/all_to_all | solution.py:81
where the time goes:
time: 161 us; the launch traced here: 160 us
  waiting for transfers between devices  70.5 us (44%)
  local copies, waits for them, and re-layouts  38.1 us (24%)
  starting transfers between devices  23.2 us (14%)
  matrix products  16.3 us (10%)
  other arithmetic  11 us (7%)
    all_to_all x2, waiting for transfers between devices, from_everyone(): return lax.all_to_all(copies, axis, split_axis=0, concat_axis=0, tiled=True)  24 us
    all_to_all x1, waiting for transfers between devices, shards(): lax.all_to_all(applied, 'band', split_axis=1, concat_axis=0, tiled=True)  23.5 us
    all_to_all x1, waiting for transfers between devices, shards(): lax.all_to_all(cell_residuals, 'band', split_axis=0, concat_axis=1, tiled...  23.1 us
    unnamed x9, local copies, waits for them, and re-layouts  9.95 us
    all_to_all x2, starting transfers between devices, from_everyone(): return lax.all_to_all(copies, axis, split_axis=0, concat_axis=0, tiled=True)  7.8 us
    dot_general x1, matrix products, apply_hamiltonian(): jnp.dot(planes, plane_table(side), preferred_element_type=jnp.float32)  7.13 us
    all_to_all x1, starting transfers between devices, shards(): lax.all_to_all(orbitals, 'band', split_axis=1, concat_axis=0, tiled=True)  6.11 us
    convert_element_type x1, other arithmetic, apply_hamiltonian(): return result.reshape(count, side * side * side).astype(jnp.bfloat16)  5.81 us
  transfers between devices with their start and end apart: 5, of which 4 were waited for; matrix products, arithmetic and copies ran while one was open for 33% of the time, Pallas kernels for 0%

commit v1 on v0

v1 whole, which is shorter than its diff:
```python
import functools

import jax
import jax.numpy as jnp
from jax import lax
from jax.experimental import pallas as pl
from jax.experimental.pallas import tpu as pltpu
from jax.sharding import PartitionSpec as P

MESH = pl.DeviceIdType.MESH
SIDE = 32
PLANE = SIDE * SIDE
LANES = 128
SLICES = PLANE // LANES
OWN = 32
BANDS = 256
PEERS = 8
DEPTH = SIDE // PEERS
OFFSETS = ((2, 1), (2, 0), (1, 1), (3, 1), (1, 0), (3, 0), (0, 1))
FIRST = 0
GATE_AT = 3


def contract_rows(left, right):
    return lax.dot_general(left, right, (((1,), (1,)), ((), ())), preferred_element_type=jnp.float32)


def kernel(
    phi_hbm, pot_hbm, out_ref, margin_ref, projected_ref,
    phi, pot, applied, block, half, margin_sum, half_sum,
    margin_send, margin_recv, proj_send, proj_recv, coef_send, coef, mixed, back,
    load_sem, phi_ss, phi_rs, margin_ss, margin_rs, proj_ss, proj_rs, coef_ss, coef_rs, back_ss, back_rs, gate,
):
    me = lax.axis_index("band")
    frag = lax.axis_index("frag")
    core = lax.rem(frag, 2)
    x, z = me // 2, lax.rem(me, 2)
    partner = frag + 1 - 2 * core

    def peer(j):
        dx, dz = OFFSETS[j]
        return lax.rem(x + dx, 4) * 2 + lax.rem(z + dz, 2)

    def source(j):
        dx, dz = OFFSETS[j]
        return lax.rem(x + 4 - dx, 4) * 2 + lax.rem(z + dz, 2)

    def rows(b):
        return pl.ds(pl.multiple_of(b * OWN, OWN), OWN)

    def cols(plane, c=0, n=PLANE):
        return pl.ds(pl.multiple_of(plane * PLANE + c * LANES, LANES), n)

    barrier = pltpu.get_barrier_semaphore()
    for j in range(PEERS - 1):
        pl.semaphore_signal(barrier, inc=1, device_id={"band": peer(j)}, device_id_type=MESH)
    pl.semaphore_signal(barrier, inc=1, device_id={"frag": partner}, device_id_type=MESH)
    loads = [pltpu.make_async_copy(pot_hbm, pot, load_sem.at[4])]
    for i in range(4):
        part = pl.ds(i * 8 * PLANE, 8 * PLANE)
        loads.append(pltpu.make_async_copy(phi_hbm.at[:, part], phi.at[:, part], load_sem.at[i]))
    for load in loads:
        load.start()
    for load in loads:
        load.wait()
    pl.semaphore_wait(barrier, PEERS)

    lane = lax.broadcasted_iota(jnp.int32, (OWN, LANES), 1)
    z_pos = lax.rem(lane, SIDE)
    z_last, z_first = z_pos == SIDE - 1, z_pos == 0
    y_inner, y_outer = lane < LANES - SIDE, lane >= SIDE

    def upper(fields):
        ahead = [pltpu.roll(f, LANES - SIDE, 1) for f in fields]
        sums = []
        for c in range(SLICES):
            y_up = jnp.where(y_inner, ahead[c], ahead[(c + 1) % SLICES])
            z_up = jnp.where(z_last, pltpu.roll(fields[c], SIDE - 1, 1), pltpu.roll(fields[c], LANES - 1, 1))
            sums.append(y_up + z_up)
        return sums

    def lower(fields):
        behind = [pltpu.roll(f, SIDE, 1) for f in fields]
        sums = []
        for c in range(SLICES):
            y_down = jnp.where(y_outer, behind[c], behind[(c - 1) % SLICES])
            z_down = jnp.where(z_first, pltpu.roll(fields[c], LANES - SIDE + 1, 1), pltpu.roll(fields[c], 1, 1))
            sums.append(y_down + z_down)
        return sums

    def phi_copy(j, k):
        plane = lax.rem(peer(j) * DEPTH + k, SIDE)
        return pltpu.make_async_remote_copy(
            src_ref=phi.at[:, cols(plane)], dst_ref=block.at[k, rows(me), :],
            send_sem=phi_ss.at[k, j], recv_sem=phi_rs.at[k, j],
            device_id={"band": peer(j)}, device_id_type=MESH)

    def phi_arrival(j, k):
        return pltpu.make_async_remote_copy(
            src_ref=phi.at[:, cols(0)], dst_ref=block.at[k, rows(source(j)), :],
            send_sem=phi_ss.at[k, j], recv_sem=phi_rs.at[k, j],
            device_id={"band": peer(j)}, device_id_type=MESH)

    def back_copy(j, k):
        return pltpu.make_async_remote_copy(
            src_ref=mixed.at[k, rows(peer(j)), :], dst_ref=back.at[k, me],
            send_sem=back_ss.at[k, j], recv_sem=back_rs.at[k, j],
            device_id={"band": peer(j)}, device_id_type=MESH)

    def back_arrival(j, k):
        return pltpu.make_async_remote_copy(
            src_ref=mixed.at[k, rows(peer(j)), :], dst_ref=back.at[k, source(j)],
            send_sem=back_ss.at[k, j], recv_sem=back_rs.at[k, j],
            device_id={"band": peer(j)}, device_id_type=MESH)

    def terms_copy(j, sent, received, ss, rs):
        return pltpu.make_async_remote_copy(
            src_ref=sent.at[rows(peer(j)), :], dst_ref=received.at[j],
            send_sem=ss.at[j], recv_sem=rs.at[j],
            device_id={"band": peer(j)}, device_id_type=MESH)

    def coef_copy(j):
        return pltpu.make_async_remote_copy(
            src_ref=coef_send, dst_ref=coef.at[rows(me), :],
            send_sem=coef_ss.at[j], recv_sem=coef_rs.at[j],
            device_id={"band": peer(j)}, device_id_type=MESH)

    def coef_arrival(j):
        return pltpu.make_async_remote_copy(
            src_ref=coef_send, dst_ref=coef.at[rows(source(j)), :],
            send_sem=coef_ss.at[j], recv_sem=coef_rs.at[j],
            device_id={"band": peer(j)}, device_id_type=MESH)

    def send_phi():
        def planes(k, carry):
            for j in range(PEERS - 1):
                phi_copy(j, k).start()
            return carry
        lax.fori_loop(0, DEPTH + 1, planes, 0)

    @pl.when(core == FIRST)
    def _():
        send_phi()

    def own_block(k, carry):
        plane = lax.rem(me * DEPTH + k, SIDE)
        block[k, rows(me), :] = phi[:, cols(plane)]
        return carry
    lax.fori_loop(0, DEPTH + 1, own_block, 0)

    def apply_plane(g, carry):
        fields = [phi[:, cols(g, c, LANES)].astype(jnp.float32) for c in range(SLICES)]
        ups, downs = upper(fields), lower(fields)
        after, before = lax.rem(g + 1, SIDE), lax.rem(g + SIDE - 1, SIDE)
        for c in range(SLICES):
            beside = ups[c] + downs[c]
            beside += phi[:, cols(after, c, LANES)].astype(jnp.float32)
            beside += phi[:, cols(before, c, LANES)].astype(jnp.float32)
            weight = pot[pl.ds(g * SLICES + c, 1), :] + 3.0
            applied[:, cols(g, c, LANES)] = (weight * fields[c] - 0.5 * beside).astype(jnp.bfloat16)
        return carry
    lax.fori_loop(0, SIDE, apply_plane, 0)

    @pl.when(core != FIRST)
    def _():
        pl.semaphore_wait(gate, 1)
        send_phi()

    def half_stencil(k, with_next):
        def some_rows(i, carry):
            r = rows(i)
            fields = [block[k, r, c * LANES:(c + 1) * LANES].astype(jnp.float32) for c in range(SLICES)]
            ups = upper(fields)
            for c in range(SLICES):
                beside = ups[c]
                if with_next:
                    beside += block[k + 1, r, c * LANES:(c + 1) * LANES].astype(jnp.float32)
                weight = 0.5 * pot[pl.ds((me * DEPTH + k) * SLICES + c, 1), :] + 1.5
                half[r, c * LANES:(c + 1) * LANES] = (weight * fields[c] - 0.5 * beside).astype(jnp.bfloat16)
            return carry
        lax.fori_loop(0, PEERS, some_rows, 0)

    for k in range(DEPTH):
        for j in range(PEERS - 1):
            phi_arrival(j, k).wait_recv()
        if k == GATE_AT:
            @pl.when(core == FIRST)
            def _():
                pl.semaphore_signal(gate, inc=1, device_id={"frag": partner}, device_id_type=MESH)
        term = contract_rows(block[k], block[k])
        margin_sum[...] = term if k == 0 else margin_sum[...] + term
        if k == DEPTH - 1:
            margin_send[...] = margin_sum[...].astype(jnp.bfloat16)
            for j in range(PEERS - 1):
                terms_copy(j, margin_send, margin_recv, margin_ss, margin_rs).start()
        if k >= 1:
            half_stencil(k - 1, True)
            term = contract_rows(block[k - 1], half[...])
            half_sum[...] = term if k == 1 else half_sum[...] + term
    half_stencil(DEPTH - 1, False)
    half_sum[...] += contract_rows(block[DEPTH - 1], half[...])
    for j in range(PEERS - 1):
        phi_arrival(j, DEPTH).wait_recv()
    total = half_sum[...] - 0.5 * contract_rows(block[DEPTH - 1], block[DEPTH])
    total = total + total.T
    half_sum[...] = total
    proj_send[...] = total.astype(jnp.bfloat16)
    for j in range(PEERS - 1):
        terms_copy(j, proj_send, proj_recv, proj_ss, proj_rs).start()

    column = lax.broadcasted_iota(jnp.int32, (OWN, BANDS), 1)
    row = lax.broadcasted_iota(jnp.int32, (OWN, BANDS), 0)
    on_diagonal = column == row + me * OWN
    margin = margin_sum[rows(me), :]
    for j in range(PEERS - 1):
        terms_copy(j, margin_send, margin_recv, margin_ss, margin_rs).wait_recv()
        margin += margin_recv[j].astype(jnp.float32)
    margin_ref[...] = margin
    diagonal = jnp.sum(jnp.where(on_diagonal, margin, 0.0), axis=1, keepdims=True)
    projected = half_sum[rows(me), :]
    for j in range(PEERS - 1):
        terms_copy(j, proj_send, proj_recv, proj_ss, proj_rs).wait_recv()
        projected += proj_recv[j].astype(jnp.float32)
    projected_ref[...] = projected
    rounded = (projected / diagonal).astype(jnp.bfloat16).astype(jnp.float32)
    own_coef = jnp.sum(jnp.where(on_diagonal, rounded, 0.0), axis=1, keepdims=True)
    others = jnp.where(on_diagonal, 0.0, rounded).astype(jnp.bfloat16)
    coef_send[...] = others
    for j in range(PEERS - 1):
        coef_copy(j).start()
    coef[rows(me), :] = others
    for j in range(PEERS - 1):
        coef_arrival(j).wait_recv()

    for k in range(DEPTH):
        mixed[k] = jnp.dot(coef[...], block[k], preferred_element_type=jnp.float32).astype(jnp.bfloat16)
        for j in range(PEERS - 1):
            back_copy(j, k).start()

    def finish(k, b, taken):
        plane = b * DEPTH + k
        for c in range(SLICES):
            rest = applied[:, cols(plane, c, LANES)].astype(jnp.float32)
            rest -= own_coef * phi[:, cols(plane, c, LANES)].astype(jnp.float32)
            out_ref[:, cols(plane, c, LANES)] = (rest - taken(c).astype(jnp.float32)).astype(jnp.bfloat16)

    def finish_own(k, carry):
        finish(k, me, lambda c: mixed[k, rows(me), c * LANES:(c + 1) * LANES])
        return carry
    lax.fori_loop(0, DEPTH, finish_own, 0)

    def finish_others(k, carry):
        for j in range(PEERS - 1):
            back_arrival(j, k).wait_recv()
            b = source(j)
            finish(k, b, lambda c: back[k, b, :, c * LANES:(c + 1) * LANES])
        return carry
    lax.fori_loop(0, DEPTH, finish_others, 0)

    for j in range(PEERS - 1):
        terms_copy(j, margin_send, margin_recv, margin_ss, margin_rs).wait_send()
        terms_copy(j, proj_send, proj_recv, proj_ss, proj_rs).wait_send()
        coef_copy(j).wait_send()

    def drain_phi(k, carry):
        for j in range(PEERS - 1):
            phi_copy(j, k).wait_send()
        return carry
    lax.fori_loop(0, DEPTH + 1, drain_phi, 0)

    def drain_back(k, carry):
        for j in range(PEERS - 1):
            back_copy(j, k).wait_send()
        return carry
    lax.fori_loop(0, DEPTH, drain_back, 0)


def shards(orbitals, potential):
    grid = orbitals.shape[1]
    bf16, f32 = jnp.bfloat16, jnp.float32
    dma = pltpu.SemaphoreType.DMA
    residuals, margin, projected = pl.pallas_call(
        kernel,
        out_shape=(
            jax.ShapeDtypeStruct((OWN, grid), bf16),
            jax.ShapeDtypeStruct((OWN, BANDS), f32),
            jax.ShapeDtypeStruct((OWN, BANDS), f32),
        ),
        in_specs=[pl.BlockSpec(memory_space=pl.ANY)] * 2,
        out_specs=[pl.BlockSpec(memory_space=pltpu.VMEM)] * 3,
        scratch_shapes=[
            pltpu.VMEM((OWN, grid), bf16),
            pltpu.VMEM((grid // LANES, LANES), f32),
            pltpu.VMEM((OWN, grid), bf16),
            pltpu.VMEM((DEPTH + 1, BANDS, PLANE), bf16),
            pltpu.VMEM((BANDS, PLANE), bf16),
            pltpu.VMEM((BANDS, BANDS), f32),
            pltpu.VMEM((BANDS, BANDS), f32),
            pltpu.VMEM((BANDS, BANDS), bf16),
            pltpu.VMEM((PEERS - 1, OWN, BANDS), bf16),
            pltpu.VMEM((BANDS, BANDS), bf16),
            pltpu.VMEM((PEERS - 1, OWN, BANDS), bf16),
            pltpu.VMEM((OWN, BANDS), bf16),
            pltpu.VMEM((BANDS, BANDS), bf16),
            pltpu.VMEM((DEPTH, BANDS, PLANE), bf16),
            pltpu.VMEM((DEPTH, PEERS, OWN, PLANE), bf16),
            dma((5,)),
            dma((DEPTH + 1, PEERS - 1)),
            dma((DEPTH + 1, PEERS - 1)),
            dma((PEERS - 1,)),
            dma((PEERS - 1,)),
            dma((PEERS - 1,)),
            dma((PEERS - 1,)),
            dma((PEERS - 1,)),
            dma((PEERS - 1,)),
            dma((DEPTH, PEERS - 1)),
            dma((DEPTH, PEERS - 1)),
            pltpu.SemaphoreType.REGULAR,
        ],
        compiler_params=pltpu.CompilerParams(collective_id=0, has_side_effects=True),
        name="subspace",
    )(orbitals, potential.reshape(grid // LANES, LANES))
    return margin, projected, residuals


def solution(mesh):
    return jax.shard_map(
        shards,
        mesh=mesh,
        in_specs=(P(("frag", "band"), None), P("frag")),
        out_specs=(P(("frag", "band"), None), P(("frag", "band"), None), P(("frag", "band"), None)),
        check_vma=False,
    )
```

time: 161 us -> 76.8 us (0.48)
  the two profiles are of different devices: /device:TPU:168 before, /device:TPU:1 now
where the time goes in v1:
time: 76.8 us; the launch traced here: 76.5 us
  Pallas kernels  70.1 us (91%)
  local copies, waits for them, and re-layouts  5.79 us (8%)
    pallas_call x1, Pallas kernels, shards(): pl.pallas_call(kernel, out_shape=(jax.ShapeDtypeStruct((OWN, grid), bf16)...  70.1 us
    unnamed x3, local copies, waits for them, and re-layouts  5.79 us

profile of v1, /device:TPU:1, one launch (start us, length us, event | category | flops | bytes accessed | tf_op | source)
XLA Modules:
  0.0 76.5 jit_solution(4812047658117944625)
XLA Ops:
  0.6 70.1 %subspace.1 = (bf16[32,32768]{1,0:T(8,128)(2,1)}, f32[32,256]{1,0:T(8,128)}, f32[32,256]{1,0:T(8,128)}) custom-call(bf16[32,32768]{1,0:T(8,128)(2,1)} %phi_hbm.1, f32[256,128]{1,0:T(8,128)} %bitcast.1), custom_call_target="tpu_custom_call" | custom-call | tf_op jit(solution)/shard_map/subspace/pallas_call | solution.py:282
  70.7 1.4 %copy.8 = f32[32,256]{1,0:T(8,128)} copy(f32[32,256]{1,0:T(8,128)} %get-tuple-element.12) | data formatting | bytes 65536
  72.1 1.4 %copy.9 = f32[32,256]{1,0:T(8,128)} copy(f32[32,256]{1,0:T(8,128)} %get-tuple-element.13) | data formatting | bytes 65536
  73.5 3.0 %copy.10 = bf16[32,32768]{1,0:T(8,128)(2,1)} copy(bf16[32,32768]{1,0:T(8,128)(2,1)} %get-tuple-element.14) | data formatting | bytes 4194304

commit v2 on v1

--- a/solution.py
+++ b/solution.py
@@ -17,8 +17,9 @@
 PEERS = 8
 DEPTH = SIDE // PEERS
 OFFSETS = ((2, 1), (2, 0), (1, 1), (3, 1), (1, 0), (3, 0), (0, 1))
-FIRST = 0
-GATE_AT = 3
+FIRST = 1
+GATE_AT = 2
+GATE_BACK_AT = 3
 
 
 def contract_rows(left, right):
@@ -28,8 +29,8 @@
 def kernel(
     phi_hbm, pot_hbm, out_ref, margin_ref, projected_ref,
     phi, pot, applied, block, half, margin_sum, half_sum,
-    margin_send, margin_recv, proj_send, proj_recv, coef_send, coef, mixed, back,
-    load_sem, phi_ss, phi_rs, margin_ss, margin_rs, proj_ss, proj_rs, coef_ss, coef_rs, back_ss, back_rs, gate,
+    terms_send, terms_recv, coef_send, coef, mixed, back,
+    load_sem, phi_ss, phi_rs, terms_ss, terms_rs, coef_ss, coef_rs, back_ss, back_rs, gate, gate_back,
 ):
     me = lax.axis_index("band")
     frag = lax.axis_index("frag")
@@ -113,10 +114,10 @@
             send_sem=back_ss.at[k, j], recv_sem=back_rs.at[k, j],
             device_id={"band": peer(j)}, device_id_type=MESH)
 
-    def terms_copy(j, sent, received, ss, rs):
-        return pltpu.make_async_remote_copy(
-            src_ref=sent.at[rows(peer(j)), :], dst_ref=received.at[j],
-            send_sem=ss.at[j], recv_sem=rs.at[j],
+    def terms_copy(j):
+        return pltpu.make_async_remote_copy(
+            src_ref=terms_send.at[rows(peer(j)), :], dst_ref=terms_recv.at[j],
+            send_sem=terms_ss.at[j], recv_sem=terms_rs.at[j],
             device_id={"band": peer(j)}, device_id_type=MESH)
 
     def coef_copy(j):
@@ -148,7 +149,8 @@
         return carry
     lax.fori_loop(0, DEPTH + 1, own_block, 0)
 
-    def apply_plane(g, carry):
+    def apply_plane(g, sums):
+        norm, energy = sums
         fields = [phi[:, cols(g, c, LANES)].astype(jnp.float32) for c in range(SLICES)]
         ups, downs = upper(fields), lower(fields)
         after, before = lax.rem(g + 1, SIDE), lax.rem(g + SIDE - 1, SIDE)
@@ -157,9 +159,15 @@
             beside += phi[:, cols(after, c, LANES)].astype(jnp.float32)
             beside += phi[:, cols(before, c, LANES)].astype(jnp.float32)
             weight = pot[pl.ds(g * SLICES + c, 1), :] + 3.0
-            applied[:, cols(g, c, LANES)] = (weight * fields[c] - 0.5 * beside).astype(jnp.bfloat16)
-        return carry
-    lax.fori_loop(0, SIDE, apply_plane, 0)
+            image = (weight * fields[c] - 0.5 * beside).astype(jnp.bfloat16)
+            applied[:, cols(g, c, LANES)] = image
+            norm += fields[c] * fields[c]
+            energy += fields[c] * image.astype(jnp.float32)
+        return norm, energy
+    zeros = jnp.zeros((OWN, LANES), jnp.float32)
+    norm, energy = lax.fori_loop(0, SIDE, apply_plane, (zeros, zeros))
+    norm = jnp.sum(norm, axis=1, keepdims=True)
+    energy = jnp.sum(energy, axis=1, keepdims=True)
 
     @pl.when(core != FIRST)
     def _():
@@ -187,12 +195,12 @@
             @pl.when(core == FIRST)
             def _():
                 pl.semaphore_signal(gate, inc=1, device_id={"frag": partner}, device_id_type=MESH)
+        if k == GATE_BACK_AT:
+            @pl.when(core != FIRST)
+            def _():
+                pl.semaphore_signal(gate_back, inc=1, device_id={"frag": partner}, device_id_type=MESH)
         term = contract_rows(block[k], block[k])
         margin_sum[...] = term if k == 0 else margin_sum[...] + term
-        if k == DEPTH - 1:
-            margin_send[...] = margin_sum[...].astype(jnp.bfloat16)
-            for j in range(PEERS - 1):
-                terms_copy(j, margin_send, margin_recv, margin_ss, margin_rs).start()
         if k >= 1:
             half_stencil(k - 1, True)
             term = contract_rows(block[k - 1], half[...])
@@ -203,46 +211,55 @@
         phi_arrival(j, DEPTH).wait_recv()
     total = half_sum[...] - 0.5 * contract_rows(block[DEPTH - 1], block[DEPTH])
     total = total + total.T
+    column = lax.broadcasted_iota(jnp.int32, (BANDS, BANDS), 1)
+    row = lax.broadcasted_iota(jnp.int32, (BANDS, BANDS), 0)
+    above, below = column > row, column < row
+    total = jnp.where(above, total, margin_sum[...])
     half_sum[...] = total
-    proj_send[...] = total.astype(jnp.bfloat16)
-    for j in range(PEERS - 1):
-        terms_copy(j, proj_send, proj_recv, proj_ss, proj_rs).start()
-
-    column = lax.broadcasted_iota(jnp.int32, (OWN, BANDS), 1)
-    row = lax.broadcasted_iota(jnp.int32, (OWN, BANDS), 0)
-    on_diagonal = column == row + me * OWN
-    margin = margin_sum[rows(me), :]
-    for j in range(PEERS - 1):
-        terms_copy(j, margin_send, margin_recv, margin_ss, margin_rs).wait_recv()
-        margin += margin_recv[j].astype(jnp.float32)
-    margin_ref[...] = margin
-    diagonal = jnp.sum(jnp.where(on_diagonal, margin, 0.0), axis=1, keepdims=True)
-    projected = half_sum[rows(me), :]
-    for j in range(PEERS - 1):
-        terms_copy(j, proj_send, proj_recv, proj_ss, proj_rs).wait_recv()
-        projected += proj_recv[j].astype(jnp.float32)
-    projected_ref[...] = projected
-    rounded = (projected / diagonal).astype(jnp.bfloat16).astype(jnp.float32)
-    own_coef = jnp.sum(jnp.where(on_diagonal, rounded, 0.0), axis=1, keepdims=True)
-    others = jnp.where(on_diagonal, 0.0, rounded).astype(jnp.bfloat16)
-    coef_send[...] = others
+    terms_send[...] = total.astype(jnp.bfloat16)
+    for j in range(PEERS - 1):
+        terms_copy(j).start()
+    own = half_sum[rows(me), :]
+    for j in range(PEERS - 1):
+        terms_copy(j).wait_recv()
+        own += terms_recv[j].astype(jnp.float32)
+    coef_send[...] = own.astype(jnp.bfloat16)
     for j in range(PEERS - 1):
         coef_copy(j).start()
-    coef[rows(me), :] = others
+    coef[rows(me), :] = own.astype(jnp.bfloat16)
     for j in range(PEERS - 1):
         coef_arrival(j).wait_recv()
+    whole = coef[...].astype(jnp.float32)
+    turned = whole.T
+    half_sum[...] = turned
+    for j in range(PEERS - 1):
+        terms_copy(j).wait_send()
+    terms_send[...] = jnp.where(above, whole, jnp.where(below, turned, 0.0)).astype(jnp.bfloat16)
 
     for k in range(DEPTH):
-        mixed[k] = jnp.dot(coef[...], block[k], preferred_element_type=jnp.float32).astype(jnp.bfloat16)
+        mixed[k] = jnp.dot(terms_send[...], block[k], preferred_element_type=jnp.float32).astype(jnp.bfloat16)
+        if k == 0:
+            @pl.when(core == FIRST)
+            def _():
+                pl.semaphore_wait(gate_back, 1)
         for j in range(PEERS - 1):
             back_copy(j, k).start()
+
+    own_column = lax.broadcasted_iota(jnp.int32, (OWN, BANDS), 1)
+    own_row = lax.broadcasted_iota(jnp.int32, (OWN, BANDS), 0) + me * OWN
+    own_turned = half_sum[rows(me), :]
+    on_diagonal = own_column == own_row
+    margin_ref[...] = jnp.where(on_diagonal, norm, jnp.where(own_column < own_row, own, own_turned))
+    projected_ref[...] = jnp.where(on_diagonal, energy, jnp.where(own_column > own_row, own, own_turned))
+    scale = 1.0 / norm
+    own_coef = energy / norm
 
     def finish(k, b, taken):
         plane = b * DEPTH + k
         for c in range(SLICES):
             rest = applied[:, cols(plane, c, LANES)].astype(jnp.float32)
             rest -= own_coef * phi[:, cols(plane, c, LANES)].astype(jnp.float32)
-            out_ref[:, cols(plane, c, LANES)] = (rest - taken(c).astype(jnp.float32)).astype(jnp.bfloat16)
+            out_ref[:, cols(plane, c, LANES)] = (rest - scale * taken(c).astype(jnp.float32)).astype(jnp.bfloat16)
 
     def finish_own(k, carry):
         finish(k, me, lambda c: mixed[k, rows(me), c * LANES:(c + 1) * LANES])
@@ -258,8 +275,6 @@
     lax.fori_loop(0, DEPTH, finish_others, 0)
 
     for j in range(PEERS - 1):
-        terms_copy(j, margin_send, margin_recv, margin_ss, margin_rs).wait_send()
-        terms_copy(j, proj_send, proj_recv, proj_ss, proj_rs).wait_send()
         coef_copy(j).wait_send()
 
     def drain_phi(k, carry):
@@ -273,6 +288,34 @@
             back_copy(j, k).wait_send()
         return carry
     lax.fori_loop(0, DEPTH, drain_back, 0)
+
+
+def put_out_kernel(res, margin, projected, res_out, margin_out, projected_out, sem):
+    copies = [
+        pltpu.make_async_copy(margin, margin_out, sem.at[4]),
+        pltpu.make_async_copy(projected, projected_out, sem.at[5]),
+    ]
+    width = res.shape[1] // 4
+    for i in range(4):
+        part = pl.ds(i * width, width)
+        copies.append(pltpu.make_async_copy(res.at[:, part], res_out.at[:, part], sem.at[i]))
+    for copy in copies:
+        copy.start()
+    for copy in copies:
+        copy.wait()
+
+
+def put_out(*arrays):
+    kept = [pltpu.with_memory_space_constraint(a, pltpu.VMEM) for a in arrays]
+    return pl.pallas_call(
+        put_out_kernel,
+        out_shape=tuple(jax.ShapeDtypeStruct(a.shape, a.dtype) for a in arrays),
+        in_specs=[pl.BlockSpec(memory_space=pltpu.VMEM)] * 3,
+        out_specs=[pl.BlockSpec(memory_space=pl.ANY)] * 3,
+        scratch_shapes=[pltpu.SemaphoreType.DMA((6,))],
+        compiler_params=pltpu.CompilerParams(vmem_limit_bytes=8 << 20),
+        name="put_out",
+    )(*kept)
 
 
 def shards(orbitals, potential):
@@ -282,11 +325,11 @@
     residuals, margin, projected = pl.pallas_call(
         kernel,
         out_shape=(
-            jax.ShapeDtypeStruct((OWN, grid), bf16),
-            jax.ShapeDtypeStruct((OWN, BANDS), f32),
-            jax.ShapeDtypeStruct((OWN, BANDS), f32),
+            pltpu.VMEM((OWN, grid), bf16),
+            pltpu.VMEM((OWN, BANDS), f32),
+            pltpu.VMEM((OWN, BANDS), f32),
         ),
-        in_specs=[pl.BlockSpec(memory_space=pl.ANY)] * 2,
+        in_specs=[pl.BlockSpec(memory_space=pltpu.HBM)] * 2,
         out_specs=[pl.BlockSpec(memory_space=pltpu.VMEM)] * 3,
         scratch_shapes=[
             pltpu.VMEM((OWN, grid), bf16),
@@ -296,8 +339,6 @@
             pltpu.VMEM((BANDS, PLANE), bf16),
             pltpu.VMEM((BANDS, BANDS), f32),
             pltpu.VMEM((BANDS, BANDS), f32),
-            pltpu.VMEM((BANDS, BANDS), bf16),
-            pltpu.VMEM((PEERS - 1, OWN, BANDS), bf16),
             pltpu.VMEM((BANDS, BANDS), bf16),
             pltpu.VMEM((PEERS - 1, OWN, BANDS), bf16),
             pltpu.VMEM((OWN, BANDS), bf16),
@@ -311,15 +352,19 @@
             dma((PEERS - 1,)),
             dma((PEERS - 1,)),
             dma((PEERS - 1,)),
-            dma((PEERS - 1,)),
-            dma((PEERS - 1,)),
             dma((DEPTH, PEERS - 1)),
             dma((DEPTH, PEERS - 1)),
             pltpu.SemaphoreType.REGULAR,
+            pltpu.SemaphoreType.REGULAR,
         ],
-        compiler_params=pltpu.CompilerParams(collective_id=0, has_side_effects=True),
+        compiler_params=pltpu.CompilerParams(
+            collective_id=0, has_side_effects=True, vmem_limit_bytes=40 << 20),
         name="subspace",
-    )(orbitals, potential.reshape(grid // LANES, LANES))
+    )(
+        pltpu.with_memory_space_constraint(orbitals, pltpu.HBM),
+        pltpu.with_memory_space_constraint(potential.reshape(grid // LANES, LANES), pltpu.HBM),
+    )
+    residuals, margin, projected = put_out(residuals, margin, projected)
     return margin, projected, residuals
 
 

time: 76.8 us -> 67.7 us (0.88)
  the two profiles are of different devices: /device:TPU:1 before, /device:TPU:6 now
where the time goes in v2:
time: 67.7 us; the launch traced here: 67.1 us
  Pallas kernels  66.5 us (98%)
    pallas_call x1, Pallas kernels, shards(): pl.pallas_call(kernel, out_shape=(pltpu.VMEM((OWN, grid), bf16), pltpu.VM...  65.1 us
    pallas_call x1, Pallas kernels, put_out(): pl.pallas_call(put_out_kernel, out_shape=tuple((jax.ShapeDtypeStruct(a.sh...  1.39 us

profile of v2, /device:TPU:6, one launch (start us, length us, event | category | flops | bytes accessed | tf_op | source)
XLA Modules:
  0.0 67.1 jit_solution(16368926113127807889)
XLA Ops:
  0.6 65.1 %subspace.1 = (bf16[32,32768]{1,0:T(8,128)(2,1)S(1)}, f32[32,256]{1,0:T(8,128)S(1)}, f32[32,256]{1,0:T(8,128)S(1)}) custom-call(bf16[32,32768]{1,0:T(8,128)(2,1)} %phi_hbm.1, f32[256,128]{1,0:T(8,128)} %bitcast.1), custom_call_target="tpu_custom_call" | custom-call | tf_op jit(solution)/shard_map/subspace/pallas_call | solution.py:325
  65.7 1.4 %put_out.1 = (bf16[32,32768]{1,0:T(8,128)(2,1)}, f32[32,256]{1,0:T(8,128)}, f32[32,256]{1,0:T(8,128)}) custom-call(bf16[32,32768]{1,0:T(8,128)(2,1)S(1)} %get-tuple-element.9.res, f32[32,256]{1,0:T(8,128)S(1)} %get-tuple-element.10.margin, f32[32,256]{1,0:T(8,128)S(1)} %get-tuple-element.11.projected), custom_call_target="tpu_custom_call" | custom-call | tf_op jit(solution)/shard_map/put_out/pallas_call | solution.py:310

commit v3 on v2

--- a/solution.py
+++ b/solution.py
@@ -15,7 +15,10 @@
 OWN = 32
 BANDS = 256
 PEERS = 8
-DEPTH = SIDE // PEERS
+DEPTH = 4
+HALF = PLANE // 2
+QUADS = HALF // LANES
+EDGE = HALF + 2 * LANES
 OFFSETS = ((2, 1), (2, 0), (1, 1), (3, 1), (1, 0), (3, 0), (0, 1))
 FIRST = 1
 GATE_AT = 2
@@ -28,9 +31,9 @@
 
 def kernel(
     phi_hbm, pot_hbm, out_ref, margin_ref, projected_ref,
-    phi, pot, applied, block, half, margin_sum, half_sum,
+    phi, pot, applied, block, half, edge_send, edge, last_rows, margin_sum, half_sum,
     terms_send, terms_recv, coef_send, coef, mixed, back,
-    load_sem, phi_ss, phi_rs, terms_ss, terms_rs, coef_ss, coef_rs, back_ss, back_rs, gate, gate_back,
+    load_sem, phi_ss, phi_rs, edge_ss, edge_rs, terms_ss, terms_rs, coef_ss, coef_rs, back_ss, back_rs, gate, gate_back,
 ):
     me = lax.axis_index("band")
     frag = lax.axis_index("frag")
@@ -49,21 +52,29 @@
     def rows(b):
         return pl.ds(pl.multiple_of(b * OWN, OWN), OWN)
 
-    def cols(plane, c=0, n=PLANE):
+    def cols(plane, c=0, n=LANES):
         return pl.ds(pl.multiple_of(plane * PLANE + c * LANES, LANES), n)
+
+    def half_cols(plane, c=0, n=LANES):
+        return pl.ds(pl.multiple_of(plane * HALF + c * LANES, LANES), n)
 
     barrier = pltpu.get_barrier_semaphore()
     for j in range(PEERS - 1):
         pl.semaphore_signal(barrier, inc=1, device_id={"band": peer(j)}, device_id_type=MESH)
     pl.semaphore_signal(barrier, inc=1, device_id={"frag": partner}, device_id_type=MESH)
-    loads = [pltpu.make_async_copy(pot_hbm, pot, load_sem.at[4])]
-    for i in range(4):
-        part = pl.ds(i * 8 * PLANE, 8 * PLANE)
-        loads.append(pltpu.make_async_copy(phi_hbm.at[:, part], phi.at[:, part], load_sem.at[i]))
-    for load in loads:
-        load.start()
-    for load in loads:
-        load.wait()
+    pot_load = pltpu.make_async_copy(pot_hbm, pot, load_sem.at[2])
+    pot_load.start()
+
+    def load_plane(plane, carry):
+        for h in range(2):
+            pltpu.make_async_copy(
+                phi_hbm.at[:, cols(plane, h * QUADS, HALF)], phi.at[h, :, half_cols(plane, 0, HALF)], load_sem.at[h],
+            ).start()
+        return carry
+    lax.fori_loop(0, SIDE, load_plane, 0)
+    for h in range(2):
+        pltpu.make_async_copy(phi_hbm.at[:, 0:SIDE * HALF], phi.at[h], load_sem.at[h]).wait()
+    pot_load.wait()
     pl.semaphore_wait(barrier, PEERS)
 
     lane = lax.broadcasted_iota(jnp.int32, (OWN, LANES), 1)
@@ -71,12 +82,13 @@
     z_last, z_first = z_pos == SIDE - 1, z_pos == 0
     y_inner, y_outer = lane < LANES - SIDE, lane >= SIDE
 
-    def upper(fields):
+    def upper(fields, beyond=None):
         ahead = [pltpu.roll(f, LANES - SIDE, 1) for f in fields]
+        after = ahead[1:] + [ahead[0] if beyond is None else beyond]
         sums = []
-        for c in range(SLICES):
-            y_up = jnp.where(y_inner, ahead[c], ahead[(c + 1) % SLICES])
-            z_up = jnp.where(z_last, pltpu.roll(fields[c], SIDE - 1, 1), pltpu.roll(fields[c], LANES - 1, 1))
+        for c, f in enumerate(fields):
+            y_up = jnp.where(y_inner, ahead[c], after[c])
+            z_up = jnp.where(z_last, pltpu.roll(f, SIDE - 1, 1), pltpu.roll(f, LANES - 1, 1))
             sums.append(y_up + z_up)
         return sums
 
@@ -90,16 +102,29 @@
         return sums
 
     def phi_copy(j, k):
-        plane = lax.rem(peer(j) * DEPTH + k, SIDE)
-        return pltpu.make_async_remote_copy(
-            src_ref=phi.at[:, cols(plane)], dst_ref=block.at[k, rows(me), :],
+        p = peer(j)
+        return pltpu.make_async_remote_copy(
+            src_ref=phi.at[lax.rem(p, 2), :, half_cols(p // 2 * PEERS + 2 * k, 0, PLANE)],
+            dst_ref=block.at[k, rows(me), :],
             send_sem=phi_ss.at[k, j], recv_sem=phi_rs.at[k, j],
-            device_id={"band": peer(j)}, device_id_type=MESH)
+            device_id={"band": p}, device_id_type=MESH)
 
     def phi_arrival(j, k):
         return pltpu.make_async_remote_copy(
-            src_ref=phi.at[:, cols(0)], dst_ref=block.at[k, rows(source(j)), :],
+            src_ref=phi.at[0, :, 0:PLANE], dst_ref=block.at[k, rows(source(j)), :],
             send_sem=phi_ss.at[k, j], recv_sem=phi_rs.at[k, j],
+            device_id={"band": peer(j)}, device_id_type=MESH)
+
+    def edge_copy(j):
+        return pltpu.make_async_remote_copy(
+            src_ref=edge_send.at[peer(j)], dst_ref=edge.at[rows(me), :],
+            send_sem=edge_ss.at[j], recv_sem=edge_rs.at[j],
+            device_id={"band": peer(j)}, device_id_type=MESH)
+
+    def edge_arrival(j):
+        return pltpu.make_async_remote_copy(
+            src_ref=edge_send.at[peer(j)], dst_ref=edge.at[rows(source(j)), :],
+            send_sem=edge_ss.at[j], recv_sem=edge_rs.at[j],
             device_id={"band": peer(j)}, device_id_type=MESH)
 
     def back_copy(j, k):
@@ -133,34 +158,57 @@
             device_id={"band": peer(j)}, device_id_type=MESH)
 
     def send_phi():
-        def planes(k, carry):
+        def chunks(k, carry):
             for j in range(PEERS - 1):
                 phi_copy(j, k).start()
             return carry
-        lax.fori_loop(0, DEPTH + 1, planes, 0)
+        lax.fori_loop(0, DEPTH, chunks, 0)
+
+    def send_edges():
+        for j in range(PEERS - 1):
+            edge_copy(j).start()
 
     @pl.when(core == FIRST)
     def _():
         send_phi()
 
+    strip = lane // SIDE
+
+    def packed(fields, at):
+        rolled = [pltpu.roll(f, (i * SIDE - at) % LANES, 1) if i * SIDE != at else f for i, f in enumerate(fields)]
+        return jnp.where(strip < 2, jnp.where(strip == 0, rolled[0], rolled[1]), jnp.where(strip == 2, rolled[2], rolled[3]))
+
+    def fill_edge(p, carry):
+        px, pz = p // 2, lax.rem(p, 2)
+        edge_send[p, :, 0:HALF] = phi[pz, :, half_cols(lax.rem(px * PEERS + PEERS, SIDE), 0, HALF)]
+        for m in range(2):
+            fields = [phi[1 - pz, :, half_cols(px * PEERS + 4 * m + i)].astype(jnp.float32) for i in range(4)]
+            edge_send[p, :, HALF + m * LANES:HALF + (m + 1) * LANES] = packed(fields, 0).astype(jnp.bfloat16)
+        return carry
+    lax.fori_loop(0, PEERS, fill_edge, 0)
+
+    @pl.when(core == FIRST)
+    def _():
+        send_edges()
+
     def own_block(k, carry):
-        plane = lax.rem(me * DEPTH + k, SIDE)
-        block[k, rows(me), :] = phi[:, cols(plane)]
-        return carry
-    lax.fori_loop(0, DEPTH + 1, own_block, 0)
+        block[k, rows(me), :] = phi[z, :, half_cols(x * PEERS + 2 * k, 0, PLANE)]
+        return carry
+    lax.fori_loop(0, DEPTH, own_block, 0)
+    edge[rows(me), :] = edge_send[me]
 
     def apply_plane(g, sums):
         norm, energy = sums
-        fields = [phi[:, cols(g, c, LANES)].astype(jnp.float32) for c in range(SLICES)]
+        def slices(plane):
+            return [phi[c // QUADS, :, half_cols(plane, c % QUADS)].astype(jnp.float32) for c in range(SLICES)]
+        fields = slices(g)
         ups, downs = upper(fields), lower(fields)
-        after, before = lax.rem(g + 1, SIDE), lax.rem(g + SIDE - 1, SIDE)
+        after, before = slices(lax.rem(g + 1, SIDE)), slices(lax.rem(g + SIDE - 1, SIDE))
         for c in range(SLICES):
-            beside = ups[c] + downs[c]
-            beside += phi[:, cols(after, c, LANES)].astype(jnp.float32)
-            beside += phi[:, cols(before, c, LANES)].astype(jnp.float32)
+            beside = ups[c] + downs[c] + after[c] + before[c]
             weight = pot[pl.ds(g * SLICES + c, 1), :] + 3.0
             image = (weight * fields[c] - 0.5 * beside).astype(jnp.bfloat16)
-            applied[:, cols(g, c, LANES)] = image
+            applied[:, cols(g, c)] = image
             norm += fields[c] * fields[c]
             energy += fields[c] * image.astype(jnp.float32)
         return norm, energy
@@ -173,20 +221,37 @@
     def _():
         pl.semaphore_wait(gate, 1)
         send_phi()
+        send_edges()
+
+    def part(c):
+        return slice(c * LANES, (c + 1) * LANES)
 
     def half_stencil(k, with_next):
         def some_rows(i, carry):
             r = rows(i)
-            fields = [block[k, r, c * LANES:(c + 1) * LANES].astype(jnp.float32) for c in range(SLICES)]
-            ups = upper(fields)
+            fields = [block[k, r, part(c)].astype(jnp.float32) for c in range(SLICES)]
+            nothing = jnp.zeros((OWN, LANES), jnp.float32)
+            ups = upper(fields[:QUADS], nothing) + upper(fields[QUADS:], nothing)
             for c in range(SLICES):
                 beside = ups[c]
-                if with_next:
-                    beside += block[k + 1, r, c * LANES:(c + 1) * LANES].astype(jnp.float32)
-                weight = 0.5 * pot[pl.ds((me * DEPTH + k) * SLICES + c, 1), :] + 1.5
-                half[r, c * LANES:(c + 1) * LANES] = (weight * fields[c] - 0.5 * beside).astype(jnp.bfloat16)
+                if c < QUADS:
+                    beside += fields[c + QUADS]
+                elif with_next:
+                    beside += block[k + 1, r, part(c - QUADS)].astype(jnp.float32)
+                plane = x * PEERS + 2 * k + c // QUADS
+                weight = 0.5 * pot[pl.ds(plane * SLICES + z * QUADS + c % QUADS, 1), :] + 1.5
+                half[r, part(c)] = (weight * fields[c] - 0.5 * beside).astype(jnp.bfloat16)
             return carry
         lax.fori_loop(0, PEERS, some_rows, 0)
+
+    def fill_last_rows(i, carry):
+        r = rows(i)
+        for m in range(2):
+            fields = [
+                block[2 * m + s // 2, r, part(s % 2 * QUADS + QUADS - 1)].astype(jnp.float32) for s in range(4)
+            ]
+            last_rows[r, part(m)] = packed(fields, LANES - SIDE).astype(jnp.bfloat16)
+        return carry
 
     for k in range(DEPTH):
         for j in range(PEERS - 1):
@@ -206,11 +271,15 @@
             term = contract_rows(block[k - 1], half[...])
             half_sum[...] = term if k == 1 else half_sum[...] + term
     half_stencil(DEPTH - 1, False)
-    half_sum[...] += contract_rows(block[DEPTH - 1], half[...])
-    for j in range(PEERS - 1):
-        phi_arrival(j, DEPTH).wait_recv()
-    total = half_sum[...] - 0.5 * contract_rows(block[DEPTH - 1], block[DEPTH])
-    total = total + total.T
+    total = half_sum[...] + contract_rows(block[DEPTH - 1], half[...])
+    half_sum[...] = total + total.T
+    lax.fori_loop(0, PEERS, fill_last_rows, 0)
+    for j in range(PEERS - 1):
+        edge_arrival(j).wait_recv()
+    inner = (block[DEPTH - 1, :, HALF:PLANE], last_rows[...])
+    outer = (edge[:, 0:HALF], edge[:, HALF:EDGE])
+    across = sum(contract_rows(a, b) + contract_rows(b, a) for a, b in zip(inner, outer))
+    total = half_sum[...] - 0.5 * across
     column = lax.broadcasted_iota(jnp.int32, (BANDS, BANDS), 1)
     row = lax.broadcasted_iota(jnp.int32, (BANDS, BANDS), 0)
     above, below = column > row, column < row
@@ -255,11 +324,13 @@
     own_coef = energy / norm
 
     def finish(k, b, taken):
-        plane = b * DEPTH + k
+        bx, bz = b // 2, lax.rem(b, 2)
         for c in range(SLICES):
-            rest = applied[:, cols(plane, c, LANES)].astype(jnp.float32)
-            rest -= own_coef * phi[:, cols(plane, c, LANES)].astype(jnp.float32)
-            out_ref[:, cols(plane, c, LANES)] = (rest - scale * taken(c).astype(jnp.float32)).astype(jnp.bfloat16)
+            plane = bx * PEERS + 2 * k + c // QUADS
+            place = cols(plane, bz * QUADS + c % QUADS)
+            rest = applied[:, place].astype(jnp.float32)
+            rest -= own_coef * phi[bz, :, half_cols(plane, c % QUADS)].astype(jnp.float32)
+            out_ref[:, place] = (rest - scale * taken(c).astype(jnp.float32)).astype(jnp.bfloat16)
 
     def finish_own(k, carry):
         finish(k, me, lambda c: mixed[k, rows(me), c * LANES:(c + 1) * LANES])
@@ -276,12 +347,13 @@
 
     for j in range(PEERS - 1):
         coef_copy(j).wait_send()
+        edge_copy(j).wait_send()
 
     def drain_phi(k, carry):
         for j in range(PEERS - 1):
             phi_copy(j, k).wait_send()
         return carry
-    lax.fori_loop(0, DEPTH + 1, drain_phi, 0)
+    lax.fori_loop(0, DEPTH, drain_phi, 0)
 
     def drain_back(k, carry):
         for j in range(PEERS - 1):
@@ -332,11 +404,14 @@
         in_specs=[pl.BlockSpec(memory_space=pltpu.HBM)] * 2,
         out_specs=[pl.BlockSpec(memory_space=pltpu.VMEM)] * 3,
         scratch_shapes=[
-            pltpu.VMEM((OWN, grid), bf16),
+            pltpu.VMEM((2, OWN, grid // 2), bf16),
             pltpu.VMEM((grid // LANES, LANES), f32),
             pltpu.VMEM((OWN, grid), bf16),
-            pltpu.VMEM((DEPTH + 1, BANDS, PLANE), bf16),
+            pltpu.VMEM((DEPTH, BANDS, PLANE), bf16),
             pltpu.VMEM((BANDS, PLANE), bf16),
+            pltpu.VMEM((PEERS, OWN, EDGE), bf16),
+            pltpu.VMEM((BANDS, EDGE), bf16),
+            pltpu.VMEM((BANDS, 2 * LANES), bf16),
             pltpu.VMEM((BANDS, BANDS), f32),
             pltpu.VMEM((BANDS, BANDS), f32),
             pltpu.VMEM((BANDS, BANDS), bf16),
@@ -345,9 +420,11 @@
             pltpu.VMEM((BANDS, BANDS), bf16),
             pltpu.VMEM((DEPTH, BANDS, PLANE), bf16),
             pltpu.VMEM((DEPTH, PEERS, OWN, PLANE), bf16),
-            dma((5,)),
-            dma((DEPTH + 1, PEERS - 1)),
-            dma((DEPTH + 1, PEERS - 1)),
+            dma((3,)),
+            dma((DEPTH, PEERS - 1)),
+            dma((DEPTH, PEERS - 1)),
+            dma((PEERS - 1,)),
+            dma((PEERS - 1,)),
             dma((PEERS - 1,)),
             dma((PEERS - 1,)),
             dma((PEERS - 1,)),

time: 67.7 us -> 67.5 us (level)
  no operation moved by 1% of the time
where the time goes in v3:
time: 67.5 us; the launch traced here: 67.1 us
  Pallas kernels  66.5 us (99%)
    pallas_call x1, Pallas kernels, shards(): pl.pallas_call(kernel, out_shape=(pltpu.VMEM((OWN, grid), bf16), pltpu.VM...  65.1 us
    pallas_call x1, Pallas kernels, put_out(): pl.pallas_call(put_out_kernel, out_shape=tuple((jax.ShapeDtypeStruct(a.sh...  1.39 us

profile of v3, /device:TPU:6, one launch (start us, length us, event | category | flops | bytes accessed | tf_op | source)
XLA Modules:
  0.0 67.1 jit_solution(5491018389785643122)
XLA Ops:
  0.6 65.1 %subspace.1 = (bf16[32,32768]{1,0:T(8,128)(2,1)S(1)}, f32[32,256]{1,0:T(8,128)S(1)}, f32[32,256]{1,0:T(8,128)S(1)}) custom-call(bf16[32,32768]{1,0:T(8,128)(2,1)} %phi_hbm.1, f32[256,128]{1,0:T(8,128)} %bitcast.1), custom_call_target="tpu_custom_call" | custom-call | tf_op jit(solution)/shard_map/subspace/pallas_call | solution.py:397
  65.8 1.4 %put_out.1 = (bf16[32,32768]{1,0:T(8,128)(2,1)}, f32[32,256]{1,0:T(8,128)}, f32[32,256]{1,0:T(8,128)}) custom-call(bf16[32,32768]{1,0:T(8,128)(2,1)S(1)} %get-tuple-element.9.res, f32[32,256]{1,0:T(8,128)S(1)} %get-tuple-element.10.margin, f32[32,256]{1,0:T(8,128)S(1)} %get-tuple-element.11.projected), custom_call_target="tpu_custom_call" | custom-call | tf_op jit(solution)/shard_map/put_out/pallas_call | solution.py:382

commit v4 on v3

--- a/solution.py
+++ b/solution.py
@@ -31,9 +31,9 @@
 
 def kernel(
     phi_hbm, pot_hbm, out_ref, margin_ref, projected_ref,
-    phi, pot, applied, block, half, edge_send, edge, last_rows, margin_sum, half_sum,
+    phi, pot, applied, sums, table, block, half, edge_send, edge, last_rows, margin_sum, half_sum,
     terms_send, terms_recv, coef_send, coef, mixed, back,
-    load_sem, phi_ss, phi_rs, edge_ss, edge_rs, terms_ss, terms_rs, coef_ss, coef_rs, back_ss, back_rs, gate, gate_back,
+    load_sem, send_sem, recv_sem, phi_rs, back_rs, last_rs, gate, gate_back,
 ):
     me = lax.axis_index("band")
     frag = lax.axis_index("frag")
@@ -106,55 +106,43 @@
         return pltpu.make_async_remote_copy(
             src_ref=phi.at[lax.rem(p, 2), :, half_cols(p // 2 * PEERS + 2 * k, 0, PLANE)],
             dst_ref=block.at[k, rows(me), :],
-            send_sem=phi_ss.at[k, j], recv_sem=phi_rs.at[k, j],
+            send_sem=send_sem.at[0], recv_sem=phi_rs.at[k],
             device_id={"band": p}, device_id_type=MESH)
-
-    def phi_arrival(j, k):
-        return pltpu.make_async_remote_copy(
-            src_ref=phi.at[0, :, 0:PLANE], dst_ref=block.at[k, rows(source(j)), :],
-            send_sem=phi_ss.at[k, j], recv_sem=phi_rs.at[k, j],
-            device_id={"band": peer(j)}, device_id_type=MESH)
 
     def edge_copy(j):
         return pltpu.make_async_remote_copy(
             src_ref=edge_send.at[peer(j)], dst_ref=edge.at[rows(me), :],
-            send_sem=edge_ss.at[j], recv_sem=edge_rs.at[j],
-            device_id={"band": peer(j)}, device_id_type=MESH)
-
-    def edge_arrival(j):
-        return pltpu.make_async_remote_copy(
-            src_ref=edge_send.at[peer(j)], dst_ref=edge.at[rows(source(j)), :],
-            send_sem=edge_ss.at[j], recv_sem=edge_rs.at[j],
+            send_sem=send_sem.at[1], recv_sem=recv_sem.at[1],
             device_id={"band": peer(j)}, device_id_type=MESH)
 
     def back_copy(j, k):
         return pltpu.make_async_remote_copy(
             src_ref=mixed.at[k, rows(peer(j)), :], dst_ref=back.at[k, me],
-            send_sem=back_ss.at[k, j], recv_sem=back_rs.at[k, j],
+            send_sem=send_sem.at[4], recv_sem=last_rs.at[j] if k == DEPTH - 1 else back_rs.at[k],
             device_id={"band": peer(j)}, device_id_type=MESH)
 
-    def back_arrival(j, k):
-        return pltpu.make_async_remote_copy(
-            src_ref=mixed.at[k, rows(peer(j)), :], dst_ref=back.at[k, source(j)],
-            send_sem=back_ss.at[k, j], recv_sem=back_rs.at[k, j],
-            device_id={"band": peer(j)}, device_id_type=MESH)
+    def all_sent(ref, i):
+        pltpu.make_async_remote_copy(
+            src_ref=ref, dst_ref=ref, send_sem=send_sem.at[i], recv_sem=recv_sem.at[0],
+            device_id={"band": peer(0)}, device_id_type=MESH).wait_send()
+
+    def all_received(ref, semaphore):
+        pltpu.make_async_remote_copy(
+            src_ref=ref, dst_ref=ref, send_sem=send_sem.at[0], recv_sem=semaphore,
+            device_id={"band": peer(0)}, device_id_type=MESH).wait_recv()
+
+    others = pl.ds(0, BANDS - OWN)
 
     def terms_copy(j):
         return pltpu.make_async_remote_copy(
             src_ref=terms_send.at[rows(peer(j)), :], dst_ref=terms_recv.at[j],
-            send_sem=terms_ss.at[j], recv_sem=terms_rs.at[j],
+            send_sem=send_sem.at[2], recv_sem=recv_sem.at[2],
             device_id={"band": peer(j)}, device_id_type=MESH)
 
     def coef_copy(j):
         return pltpu.make_async_remote_copy(
             src_ref=coef_send, dst_ref=coef.at[rows(me), :],
-            send_sem=coef_ss.at[j], recv_sem=coef_rs.at[j],
-            device_id={"band": peer(j)}, device_id_type=MESH)
-
-    def coef_arrival(j):
-        return pltpu.make_async_remote_copy(
-            src_ref=coef_send, dst_ref=coef.at[rows(source(j)), :],
-            send_sem=coef_ss.at[j], recv_sem=coef_rs.at[j],
+            send_sem=send_sem.at[3], recv_sem=recv_sem.at[3],
             device_id={"band": peer(j)}, device_id_type=MESH)
 
     def send_phi():
@@ -197,8 +185,8 @@
     lax.fori_loop(0, DEPTH, own_block, 0)
     edge[rows(me), :] = edge_send[me]
 
-    def apply_plane(g, sums):
-        norm, energy = sums
+    def apply_plane(g, carry):
+        norm, energy = carry
         def slices(plane):
             return [phi[c // QUADS, :, half_cols(plane, c % QUADS)].astype(jnp.float32) for c in range(SLICES)]
         fields = slices(g)
@@ -212,13 +200,28 @@
             norm += fields[c] * fields[c]
             energy += fields[c] * image.astype(jnp.float32)
         return norm, energy
-    zeros = jnp.zeros((OWN, LANES), jnp.float32)
-    norm, energy = lax.fori_loop(0, SIDE, apply_plane, (zeros, zeros))
-    norm = jnp.sum(norm, axis=1, keepdims=True)
-    energy = jnp.sum(energy, axis=1, keepdims=True)
+
+    def apply_planes(first, last):
+        zeros = jnp.zeros((OWN, LANES), jnp.float32)
+        norm, energy = lax.fori_loop(first, last, apply_plane, (zeros, zeros))
+        sums[0] = norm if first == 0 else sums[0] + norm
+        sums[1] = energy if first == 0 else sums[1] + energy
+
+    def fill_table(i, carry):
+        there = lax.broadcasted_iota(jnp.int32, (SIDE, HALF), 0)
+        here = lax.broadcasted_iota(jnp.int32, (SIDE, HALF), 1)
+        here_y, here_z = here // SIDE, lax.rem(here, SIDE)
+        same_y, same_z = here_y == i, there == here_z
+        up_z = same_y & (there == lax.rem(here_z + 1, SIDE))
+        up_y = (here_y == i - 1) & same_z
+        values = jnp.where(same_y & same_z, 1.5, 0.0) - jnp.where(up_z | up_y, 0.5, 0.0)
+        table[rows(i), :] = values.astype(jnp.bfloat16)
+        return carry
+    lax.fori_loop(0, HALF // SIDE, fill_table, 0)
 
     @pl.when(core != FIRST)
     def _():
+        apply_planes(0, SIDE)
         pl.semaphore_wait(gate, 1)
         send_phi()
         send_edges()
@@ -226,36 +229,30 @@
     def part(c):
         return slice(c * LANES, (c + 1) * LANES)
 
-    def half_stencil(k, with_next):
+    def half_stencil(k):
+        for u in range(2):
+            plane = x * PEERS + 2 * k + u
+            inside = jnp.dot(block[k, :, u * HALF:(u + 1) * HALF], table[...], preferred_element_type=jnp.float32)
+            for c in range(QUADS):
+                here = part(u * QUADS + c)
+                weight = 0.5 * pot[pl.ds(plane * SLICES + z * QUADS + c, 1), :]
+                value = inside[:, part(c)] + weight * block[k, :, here].astype(jnp.float32)
+                if u == 0:
+                    value -= 0.5 * block[k, :, part(QUADS + c)].astype(jnp.float32)
+                half[:, here] = value.astype(jnp.bfloat16)
+
+    def fill_last_rows(m):
         def some_rows(i, carry):
             r = rows(i)
-            fields = [block[k, r, part(c)].astype(jnp.float32) for c in range(SLICES)]
-            nothing = jnp.zeros((OWN, LANES), jnp.float32)
-            ups = upper(fields[:QUADS], nothing) + upper(fields[QUADS:], nothing)
-            for c in range(SLICES):
-                beside = ups[c]
-                if c < QUADS:
-                    beside += fields[c + QUADS]
-                elif with_next:
-                    beside += block[k + 1, r, part(c - QUADS)].astype(jnp.float32)
-                plane = x * PEERS + 2 * k + c // QUADS
-                weight = 0.5 * pot[pl.ds(plane * SLICES + z * QUADS + c % QUADS, 1), :] + 1.5
-                half[r, part(c)] = (weight * fields[c] - 0.5 * beside).astype(jnp.bfloat16)
-            return carry
-        lax.fori_loop(0, PEERS, some_rows, 0)
-
-    def fill_last_rows(i, carry):
-        r = rows(i)
-        for m in range(2):
             fields = [
                 block[2 * m + s // 2, r, part(s % 2 * QUADS + QUADS - 1)].astype(jnp.float32) for s in range(4)
             ]
             last_rows[r, part(m)] = packed(fields, LANES - SIDE).astype(jnp.bfloat16)
-        return carry
+            return carry
+        lax.fori_loop(0, PEERS, some_rows, 0)
 
     for k in range(DEPTH):
-        for j in range(PEERS - 1):
-            phi_arrival(j, k).wait_recv()
+        all_received(block.at[k, others, :], phi_rs.at[k])
         if k == GATE_AT:
             @pl.when(core == FIRST)
             def _():
@@ -266,16 +263,15 @@
                 pl.semaphore_signal(gate_back, inc=1, device_id={"frag": partner}, device_id_type=MESH)
         term = contract_rows(block[k], block[k])
         margin_sum[...] = term if k == 0 else margin_sum[...] + term
+        half_stencil(k)
+        term = contract_rows(block[k], half[...])
         if k >= 1:
-            half_stencil(k - 1, True)
-            term = contract_rows(block[k - 1], half[...])
-            half_sum[...] = term if k == 1 else half_sum[...] + term
-    half_stencil(DEPTH - 1, False)
-    total = half_sum[...] + contract_rows(block[DEPTH - 1], half[...])
-    half_sum[...] = total + total.T
-    lax.fori_loop(0, PEERS, fill_last_rows, 0)
-    for j in range(PEERS - 1):
-        edge_arrival(j).wait_recv()
+            term -= 0.5 * contract_rows(block[k - 1, :, HALF:PLANE], block[k, :, 0:HALF])
+        half_sum[...] = term if k == 0 else half_sum[...] + term
+        if k % 2 == 1:
+            fill_last_rows(k // 2)
+    half_sum[...] = half_sum[...] + half_sum[...].T
+    all_received(edge.at[others, :], recv_sem.at[1])
     inner = (block[DEPTH - 1, :, HALF:PLANE], last_rows[...])
     outer = (edge[:, 0:HALF], edge[:, HALF:EDGE])
     across = sum(contract_rows(a, b) + contract_rows(b, a) for a, b in zip(inner, outer))
@@ -288,21 +284,29 @@
     terms_send[...] = total.astype(jnp.bfloat16)
     for j in range(PEERS - 1):
         terms_copy(j).start()
+
+    @pl.when(core == FIRST)
+    def _():
+        apply_planes(0, SIDE // 2)
+
     own = half_sum[rows(me), :]
+    all_received(terms_recv, recv_sem.at[2])
     for j in range(PEERS - 1):
-        terms_copy(j).wait_recv()
         own += terms_recv[j].astype(jnp.float32)
     coef_send[...] = own.astype(jnp.bfloat16)
     for j in range(PEERS - 1):
         coef_copy(j).start()
     coef[rows(me), :] = own.astype(jnp.bfloat16)
-    for j in range(PEERS - 1):
-        coef_arrival(j).wait_recv()
+
+    @pl.when(core == FIRST)
+    def _():
+        apply_planes(SIDE // 2, SIDE)
+
+    all_received(coef.at[others, :], recv_sem.at[3])
     whole = coef[...].astype(jnp.float32)
     turned = whole.T
     half_sum[...] = turned
-    for j in range(PEERS - 1):
-        terms_copy(j).wait_send()
+    all_sent(terms_send.at[others, :], 2)
     terms_send[...] = jnp.where(above, whole, jnp.where(below, turned, 0.0)).astype(jnp.bfloat16)
 
     for k in range(DEPTH):
@@ -314,6 +318,8 @@
         for j in range(PEERS - 1):
             back_copy(j, k).start()
 
+    norm = jnp.sum(sums[0], axis=1, keepdims=True)
+    energy = jnp.sum(sums[1], axis=1, keepdims=True)
     own_column = lax.broadcasted_iota(jnp.int32, (OWN, BANDS), 1)
     own_row = lax.broadcasted_iota(jnp.int32, (OWN, BANDS), 0) + me * OWN
     own_turned = half_sum[rows(me), :]
@@ -337,29 +343,24 @@
         return carry
     lax.fori_loop(0, DEPTH, finish_own, 0)
 
+    def finish_from(k, j):
+        b = source(j)
+        finish(k, b, lambda c: back[k, b, :, c * LANES:(c + 1) * LANES])
+
     def finish_others(k, carry):
+        all_received(back.at[k, pl.ds(0, PEERS - 1)], back_rs.at[k])
         for j in range(PEERS - 1):
-            back_arrival(j, k).wait_recv()
-            b = source(j)
-            finish(k, b, lambda c: back[k, b, :, c * LANES:(c + 1) * LANES])
-        return carry
-    lax.fori_loop(0, DEPTH, finish_others, 0)
-
+            finish_from(k, j)
+        return carry
+    lax.fori_loop(0, DEPTH - 1, finish_others, 0)
     for j in range(PEERS - 1):
-        coef_copy(j).wait_send()
-        edge_copy(j).wait_send()
-
-    def drain_phi(k, carry):
-        for j in range(PEERS - 1):
-            phi_copy(j, k).wait_send()
-        return carry
-    lax.fori_loop(0, DEPTH, drain_phi, 0)
-
-    def drain_back(k, carry):
-        for j in range(PEERS - 1):
-            back_copy(j, k).wait_send()
-        return carry
-    lax.fori_loop(0, DEPTH, drain_back, 0)
+        all_received(back.at[DEPTH - 1, source(j)], last_rs.at[j])
+        finish_from(DEPTH - 1, j)
+
+    all_sent(block.at[:, others, :], 0)
+    all_sent(edge.at[others, :], 1)
+    all_sent(coef.at[others, :], 3)
+    all_sent(mixed.at[:, others, :], 4)
 
 
 def put_out_kernel(res, margin, projected, res_out, margin_out, projected_out, sem):
@@ -407,6 +408,8 @@
             pltpu.VMEM((2, OWN, grid // 2), bf16),
             pltpu.VMEM((grid // LANES, LANES), f32),
             pltpu.VMEM((OWN, grid), bf16),
+            pltpu.VMEM((2, OWN, LANES), f32),
+            pltpu.VMEM((HALF, HALF), bf16),
             pltpu.VMEM((DEPTH, BANDS, PLANE), bf16),
             pltpu.VMEM((BANDS, PLANE), bf16),
             pltpu.VMEM((PEERS, OWN, EDGE), bf16),
@@ -421,16 +424,11 @@
             pltpu.VMEM((DEPTH, BANDS, PLANE), bf16),
             pltpu.VMEM((DEPTH, PEERS, OWN, PLANE), bf16),
             dma((3,)),
-            dma((DEPTH, PEERS - 1)),
-            dma((DEPTH, PEERS - 1)),
+            dma((5,)),
+            dma((4,)),
+            dma((DEPTH,)),
+            dma((DEPTH - 1,)),
             dma((PEERS - 1,)),
-            dma((PEERS - 1,)),
-            dma((PEERS - 1,)),
-            dma((PEERS - 1,)),
-            dma((PEERS - 1,)),
-            dma((PEERS - 1,)),
-            dma((DEPTH, PEERS - 1)),
-            dma((DEPTH, PEERS - 1)),
             pltpu.SemaphoreType.REGULAR,
             pltpu.SemaphoreType.REGULAR,
         ],

time: 67.5 us -> 65 us (0.963)
  Pallas kernels: 66.5 us -> 64.2 us
    pallas_call x1, Pallas kernels: 65.1 us -> 62.8 us  [shards(): pl.pallas_call(kernel, out_shape=(pltpu.VMEM((OWN, grid), bf16), pltpu.VM...]
where the time goes in v4:
time: 65 us; the launch traced here: 64.8 us
  Pallas kernels  64.2 us (99%)
    pallas_call x1, Pallas kernels, shards(): pl.pallas_call(kernel, out_shape=(pltpu.VMEM((OWN, grid), bf16), pltpu.VM...  62.8 us
    pallas_call x1, Pallas kernels, put_out(): pl.pallas_call(put_out_kernel, out_shape=tuple((jax.ShapeDtypeStruct(a.sh...  1.39 us

profile of v4, /device:TPU:6, one launch (start us, length us, event | category | flops | bytes accessed | tf_op | source)
XLA Modules:
  0.0 64.8 jit_solution(975012150086778209)
XLA Ops:
  0.6 62.8 %subspace.1 = (bf16[32,32768]{1,0:T(8,128)(2,1)S(1)}, f32[32,256]{1,0:T(8,128)S(1)}, f32[32,256]{1,0:T(8,128)S(1)}) custom-call(bf16[32,32768]{1,0:T(8,128)(2,1)} %phi_hbm.1, f32[256,128]{1,0:T(8,128)} %bitcast.1), custom_call_target="tpu_custom_call" | custom-call | tf_op jit(solution)/shard_map/subspace/pallas_call | solution.py:398
  63.4 1.4 %put_out.1 = (bf16[32,32768]{1,0:T(8,128)(2,1)}, f32[32,256]{1,0:T(8,128)}, f32[32,256]{1,0:T(8,128)}) custom-call(bf16[32,32768]{1,0:T(8,128)(2,1)S(1)} %get-tuple-element.9.res, f32[32,256]{1,0:T(8,128)S(1)} %get-tuple-element.10.margin, f32[32,256]{1,0:T(8,128)S(1)} %get-tuple-element.11.projected), custom_call_target="tpu_custom_call" | custom-call | tf_op jit(solution)/shard_map/put_out/pallas_call | solution.py:383

commit v5 on v4

--- a/solution.py
+++ b/solution.py
@@ -31,7 +31,7 @@
 
 def kernel(
     phi_hbm, pot_hbm, out_ref, margin_ref, projected_ref,
-    phi, pot, applied, sums, table, block, half, edge_send, edge, last_rows, margin_sum, half_sum,
+    phi, pot, applied, sums, table, block, half, edge_send, edge, surface, margin_sum, half_sum,
     terms_send, terms_recv, coef_send, coef, mixed, back,
     load_sem, send_sem, recv_sem, phi_rs, back_rs, last_rs, gate, gate_back,
 ):
@@ -115,9 +115,9 @@
             send_sem=send_sem.at[1], recv_sem=recv_sem.at[1],
             device_id={"band": peer(j)}, device_id_type=MESH)
 
-    def back_copy(j, k):
+    def back_copy(j, k, here):
         return pltpu.make_async_remote_copy(
-            src_ref=mixed.at[k, rows(peer(j)), :], dst_ref=back.at[k, me],
+            src_ref=mixed.at[k, rows(peer(j)), here], dst_ref=back.at[k, me, :, here],
             send_sem=send_sem.at[4], recv_sem=last_rs.at[j] if k == DEPTH - 1 else back_rs.at[k],
             device_id={"band": peer(j)}, device_id_type=MESH)
 
@@ -247,7 +247,7 @@
             fields = [
                 block[2 * m + s // 2, r, part(s % 2 * QUADS + QUADS - 1)].astype(jnp.float32) for s in range(4)
             ]
-            last_rows[r, part(m)] = packed(fields, LANES - SIDE).astype(jnp.bfloat16)
+            surface[r, part(QUADS + m)] = packed(fields, LANES - SIDE).astype(jnp.bfloat16)
             return carry
         lax.fori_loop(0, PEERS, some_rows, 0)
 
@@ -271,10 +271,9 @@
         if k % 2 == 1:
             fill_last_rows(k // 2)
     half_sum[...] = half_sum[...] + half_sum[...].T
+    surface[:, 0:HALF] = block[DEPTH - 1, :, HALF:PLANE]
     all_received(edge.at[others, :], recv_sem.at[1])
-    inner = (block[DEPTH - 1, :, HALF:PLANE], last_rows[...])
-    outer = (edge[:, 0:HALF], edge[:, HALF:EDGE])
-    across = sum(contract_rows(a, b) + contract_rows(b, a) for a, b in zip(inner, outer))
+    across = contract_rows(surface[...], edge[...]) + contract_rows(edge[...], surface[...])
     total = half_sum[...] - 0.5 * across
     column = lax.broadcasted_iota(jnp.int32, (BANDS, BANDS), 1)
     row = lax.broadcasted_iota(jnp.int32, (BANDS, BANDS), 0)
@@ -309,14 +308,15 @@
     all_sent(terms_send.at[others, :], 2)
     terms_send[...] = jnp.where(above, whole, jnp.where(below, turned, 0.0)).astype(jnp.bfloat16)
 
-    for k in range(DEPTH):
-        mixed[k] = jnp.dot(terms_send[...], block[k], preferred_element_type=jnp.float32).astype(jnp.bfloat16)
-        if k == 0:
+    for k, here in [(0, pl.ds(0, HALF)), (0, pl.ds(HALF, HALF))] + [(k, pl.ds(0, PLANE)) for k in range(1, DEPTH)]:
+        mixed[k, :, here] = jnp.dot(
+            terms_send[...], block[k, :, here], preferred_element_type=jnp.float32).astype(jnp.bfloat16)
+        if (k, here.start) == (0, 0):
             @pl.when(core == FIRST)
             def _():
                 pl.semaphore_wait(gate_back, 1)
         for j in range(PEERS - 1):
-            back_copy(j, k).start()
+            back_copy(j, k, here).start()
 
     norm = jnp.sum(sums[0], axis=1, keepdims=True)
     energy = jnp.sum(sums[1], axis=1, keepdims=True)
@@ -364,18 +364,19 @@
 
 
 def put_out_kernel(res, margin, projected, res_out, margin_out, projected_out, sem):
-    copies = [
-        pltpu.make_async_copy(margin, margin_out, sem.at[4]),
-        pltpu.make_async_copy(projected, projected_out, sem.at[5]),
-    ]
     width = res.shape[1] // 4
     for i in range(4):
         part = pl.ds(i * width, width)
-        copies.append(pltpu.make_async_copy(res.at[:, part], res_out.at[:, part], sem.at[i]))
-    for copy in copies:
+        pltpu.make_async_copy(res.at[:, part], res_out.at[:, part], sem.at[0]).start()
+    small = [
+        pltpu.make_async_copy(margin, margin_out, sem.at[1]),
+        pltpu.make_async_copy(projected, projected_out, sem.at[2]),
+    ]
+    for copy in small:
         copy.start()
-    for copy in copies:
+    for copy in small:
         copy.wait()
+    pltpu.make_async_copy(res, res_out, sem.at[0]).wait()
 
 
 def put_out(*arrays):
@@ -385,7 +386,7 @@
         out_shape=tuple(jax.ShapeDtypeStruct(a.shape, a.dtype) for a in arrays),
         in_specs=[pl.BlockSpec(memory_space=pltpu.VMEM)] * 3,
         out_specs=[pl.BlockSpec(memory_space=pl.ANY)] * 3,
-        scratch_shapes=[pltpu.SemaphoreType.DMA((6,))],
+        scratch_shapes=[pltpu.SemaphoreType.DMA((3,))],
         compiler_params=pltpu.CompilerParams(vmem_limit_bytes=8 << 20),
         name="put_out",
     )(*kept)
@@ -414,7 +415,7 @@
             pltpu.VMEM((BANDS, PLANE), bf16),
             pltpu.VMEM((PEERS, OWN, EDGE), bf16),
             pltpu.VMEM((BANDS, EDGE), bf16),
-            pltpu.VMEM((BANDS, 2 * LANES), bf16),
+            pltpu.VMEM((BANDS, EDGE), bf16),
             pltpu.VMEM((BANDS, BANDS), f32),
             pltpu.VMEM((BANDS, BANDS), f32),
             pltpu.VMEM((BANDS, BANDS), bf16),

time: 65 us -> 64.8 us (level)
  no operation moved by 1% of the time
where the time goes in v5:
time: 64.8 us; the launch traced here: 64.5 us
  Pallas kernels  63.8 us (98%)
    pallas_call x1, Pallas kernels, shards(): pl.pallas_call(kernel, out_shape=(pltpu.VMEM((OWN, grid), bf16), pltpu.VM...  62.5 us
    pallas_call x1, Pallas kernels, put_out(): pl.pallas_call(put_out_kernel, out_shape=tuple((jax.ShapeDtypeStruct(a.sh...  1.35 us

profile of v5, /device:TPU:6, one launch (start us, length us, event | category | flops | bytes accessed | tf_op | source)
XLA Modules:
  0.0 64.5 jit_solution(10065039682078354063)
XLA Ops:
  0.6 62.5 %subspace.1 = (bf16[32,32768]{1,0:T(8,128)(2,1)S(1)}, f32[32,256]{1,0:T(8,128)S(1)}, f32[32,256]{1,0:T(8,128)S(1)}) custom-call(bf16[32,32768]{1,0:T(8,128)(2,1)} %phi_hbm.1, f32[256,128]{1,0:T(8,128)} %bitcast.1), custom_call_target="tpu_custom_call" | custom-call | tf_op jit(solution)/shard_map/subspace/pallas_call | solution.py:399
  63.1 1.3 %put_out.1 = (bf16[32,32768]{1,0:T(8,128)(2,1)}, f32[32,256]{1,0:T(8,128)}, f32[32,256]{1,0:T(8,128)}) custom-call(bf16[32,32768]{1,0:T(8,128)(2,1)S(1)} %get-tuple-element.9.res, f32[32,256]{1,0:T(8,128)S(1)} %get-tuple-element.10.margin, f32[32,256]{1,0:T(8,128)S(1)} %get-tuple-element.11.projected), custom_call_target="tpu_custom_call" | custom-call | tf_op jit(solution)/shard_map/put_out/pallas_call | solution.py:384
